TPU v7x, 32 devices: a whole 2x2x4 slice. The times are simulated.
32 devices in a mesh: groups: 2 (over y), expert: 4 (over x, core), etp: 4 (over z).
Axes of the slice: x: 2, y: 2, z: 4, core: 2. Of those that a mesh axis runs over, the one named last changes fastest.
Arguments:
- tokens: bfloat16 [1024, 4096], P(('groups', 'expert'), 'etp'), parts along dimension 0, may hold values from -6 to 6
- route_ids: int32 [1024, 2], P(('groups', 'expert')), parts along dimension 0, may hold values from 0 to 3, all different within a row; in each aligned block of 128 rows (0 to 127, 128 to 255, ...) at most 96 rows name the same one
- gate_weights: float32 [1024, 2], P(('groups', 'expert')), parts along dimension 0, may hold values from 0.2 to 1
- w_gate: bfloat16 [4, 4096, 14336], P('expert', None, 'etp'), may hold values from -0.09375 to 0.09375
- w_up: bfloat16 [4, 4096, 14336], P('expert', None, 'etp'), may hold values from -0.09375 to 0.09375
- w_down: bfloat16 [4, 14336, 4096], P('expert', 'etp'), may hold values from -0.0625 to 0.0625
Outputs:
- mixed: bfloat16 [1024, 4096], P(('groups', 'expert'), 'etp'), parts along dimension 0
There are 2 independent parts, one for each index of `groups`. A program takes and returns all parts, laid end to end along the dimension named above; an argument that names none is the same for every part. Nothing has to cross between parts.
Inputs may be any that keep to these rules, and one draw needn't show every extreme that they name: `route_ids`: each row names two different experts. In the rows of one index of expert (128 aligned rows), no expert is named by more than 96 rows, a bound that some block reaches.
All inputs are finite; a program needn't handle non-finite values.
Results may differ from a plain program's by a relative error of at most 0.024.
Values may be sent and summed in bfloat16 or wider, within the bound.
A program may use at most 192 MiB of HBM per device.

v0:
```python
import jax
import jax.numpy as jnp
from jax import lax
from jax.sharding import PartitionSpec as P

CAP = 96


def shards(tokens, route_ids, gate_weights, w_gate, w_up, w_down):
    cycle_size = lax.axis_size("expert")
    token_count, local_width = tokens.shape
    slot_total = cycle_size * CAP
    expert_iota = lax.broadcasted_iota(jnp.int32, (1, 1, cycle_size), 2)
    hit_mask = route_ids[:, :, None] == expert_iota
    routed = jnp.any(hit_mask, axis=1).astype(jnp.int32)
    weighting = jnp.sum(jnp.where(hit_mask, gate_weights[:, :, None], 0.0), axis=1)
    slot_index = jnp.cumsum(routed, axis=0) - 1
    expert_base = lax.broadcasted_iota(jnp.int32, (1, cycle_size), 1) * CAP
    target_slot = jnp.where(routed == 1, expert_base + slot_index, -1)
    slot_iota = lax.broadcasted_iota(jnp.int32, (1, 1, slot_total), 2)
    pick_table = target_slot[:, :, None] == slot_iota
    select_table = jnp.any(pick_table, axis=1).astype(jnp.bfloat16)
    combine_table = jnp.sum(jnp.where(pick_table, weighting[:, :, None], 0.0), axis=1)
    dispatched = jnp.dot(select_table.T, tokens, preferred_element_type=jnp.float32)
    dispatched = dispatched.astype(jnp.bfloat16).reshape(cycle_size, CAP, local_width)
    gate_local = w_gate[0]
    up_local = w_up[0]
    down_local = w_down[0]
    received = lax.all_to_all(dispatched, "expert", split_axis=0, concat_axis=0, tiled=True)
    columns_in = lax.all_gather(
        received.reshape(slot_total, local_width), "etp", axis=1, tiled=True
    )
    gate_sum = jnp.dot(columns_in, gate_local, preferred_element_type=jnp.float32)
    up_sum = jnp.dot(columns_in, up_local, preferred_element_type=jnp.float32)
    hidden = (jax.nn.silu(gate_sum) * up_sum).astype(jnp.bfloat16)
    partial_out = jnp.dot(hidden, down_local, preferred_element_type=jnp.float32).astype(
        jnp.bfloat16
    )
    finished = (
        lax.psum_scatter(partial_out, "etp", scatter_dimension=1, tiled=True)
        .astype(jnp.float32)
        .astype(jnp.bfloat16)
    )
    results = lax.all_to_all(
        finished.reshape(cycle_size, CAP, local_width),
        "expert",
        split_axis=0,
        concat_axis=0,
        tiled=True,
    )
    flat_results = results.reshape(slot_total, local_width).astype(jnp.float32)
    mixed = jnp.dot(combine_table, flat_results, precision=lax.Precision.HIGHEST)
    return mixed.astype(jnp.bfloat16)


def solution(mesh):
    return jax.shard_map(
        shards,
        mesh=mesh,
        in_specs=(
            P(("groups", "expert"), "etp"),
            P(("groups", "expert"), None),
            P(("groups", "expert"), None),
            P("expert", None, "etp"),
            P("expert", None, "etp"),
            P("expert", "etp", None),
        ),
        out_specs=P(("groups", "expert"), "etp"),
        check_vma=False,
    )
```

profile of v0, /device:TPU:0, one launch (start us, length us, event | category | flops | bytes accessed | tf_op | source)
XLA Modules:
  0.0 231.4 jit_solution(1056805115542354805)
XLA Ops:
  6.5 0.0 copy-start
  6.5 0.0 all-gather.2.cloned.1.call-start
  6.5 0.7 fusion.18
  7.3 0.1 copy.14
  7.4 0.2 reduce_window_sum.11
  7.6 0.1 copy.15
  7.6 0.1 add_select_fusion
  7.7 0.2 fusion.17
  7.9 0.0 copy-done
  7.9 0.4 convolution_convert_fusion
  8.3 15.8 %all_to_all.10 = bf16[4,96,1024]{2,1,0:T(8,128)(2,1)} all-to-all(bf16[4,96,1024]{2,1,0:T(8,128)(2,1)S(1)} %bitcast.37), channel_id=1, replica_groups=mesh['groups'=2,'expert'=4,'etp'=4] {'expert'}, dimensions={0} | all-to-all | bytes 1572864 | tf_op jit(solution)/shard_map/all_to_all | solution.py:29
  24.1 0.0 all-gather.2.cloned.1.call-update
  24.1 0.0 reduce-scatter.2.cloned.1.call-start
  24.2 64.3 %all-gather.2.cloned.1.call-done = bf16[384,4096]{1,0:T(8,128)(2,1)} async-done(((bf16[384,1024]{1,0:T(8,128)(2,1)}), bf16[384,4096]{1,0:T(8,128)(2,1)}) %all-gather.2.cloned.1.call-update) | async-done | bytes 3145744 | tf_op jit(solution)/shard_map/all_gather | solution.py:30
  88.5 0.0 copy-start.4
  88.5 23.5 %fusion.4 = f32[384,3584]{1,0:T(8,128)} fusion(bf16[384,4096]{1,0:T(8,128)(2,1)} %all-gather.2.cloned.1.call-done, bf16[1,4096,3584]{2,1,0:T(8,128)(2,1)} %param.9), kind=kOutput, calls=%fused_computation.4 | convolution fusion | flops 11274289152 | bytes 38010880 | tf_op jit(solution)/shard_map/dot_general | solution.py:33
  112.0 0.0 copy-done.4
  112.0 18.2 %fusion.12.clone.4 = bf16[384,3584]{1,0:T(8,128)(2,1)S(1)} fusion(bf16[384,4096]{1,0:T(8,128)(2,1)S(1)} %copy-done.4, bf16[1,4096,3584]{2,1,0:T(8,128)(2,1)} %param.10, f32[384,3584]{1,0:T(8,128)} %fusion.4), kind=kOutput, calls=%fused_computation.8.clone.clone.clone.1 | convolution fusion | flops 11282546688 | bytes 40763392 | tf_op jit(solution)/shard_map/dot_general | solution.py:34
  130.2 0.0 copy-start.2
  130.2 0.0 copy-start.3
  130.2 0.0 copy-start.1
  130.2 18.7 %fusion.9 = bf16[384,4096]{1,0:T(8,128)(2,1)} fusion(bf16[1,3584,4096]{2,1,0:T(8,128)(2,1)} %param.11, bf16[384,3584]{1,0:T(8,128)(2,1)S(1)} %fusion.12.clone.4), kind=kOutput, calls=%fused_computation.7 | convolution fusion | flops 11275862016 | bytes 35258368 | tf_op jit(solution)/shard_map/dot_general | solution.py:36
  149.0 0.0 reduce-scatter.2.cloned.1.call-update
  149.0 59.2 %reduce-scatter.2.cloned.1.call-done = bf16[384,1024]{1,0:T(8,128)(2,1)} async-done(((bf16[384,4096]{1,0:T(8,128)(2,1)}), bf16[384,1024]{1,0:T(8,128)(2,1)}) %reduce-scatter.2.cloned.1.call-update) | async-done | bytes 786448 | tf_op jit(solution)/shard_map/reduce_scatter | solution.py:40
  208.2 3.5 %all-to-all-start.1 = ((bf16[4,96,1024]{2,1,0:T(8,128)(2,1)}), bf16[4,96,1024]{2,1,0:T(8,128)(2,1)S(1)}, u32[]{:S(2)}, u32[]{:S(2)}) async-start(bf16[4,96,1024]{2,1,0:T(8,128)(2,1)} %bitcast.38), calls=%async_computation.2 | async-start | bytes 1572864 | tf_op jit(solution)/shard_map/all_to_all | solution.py:44
  211.7 0.0 copy-done.2
  211.7 0.0 copy-done.3
  211.7 0.2 select_reduce_fusion
  211.9 11.3 %all-to-all-done.1 = bf16[4,96,1024]{2,1,0:T(8,128)(2,1)S(1)} async-done(((bf16[4,96,1024]{2,1,0:T(8,128)(2,1)}), bf16[4,96,1024]{2,1,0:T(8,128)(2,1)S(1)}, u32[]{:S(2)}, u32[]{:S(2)}) %all-to-all-start.1) | async-done | bytes 786464 | tf_op jit(solution)/shard_map/all_to_all | solution.py:44
  223.3 1.3 convolution_convert_fusion.1
  224.6 0.0 copy-done.1
  (3 shorter events, 0.0 us)
Async XLA Ops:
  6.5 1.4 copy-start
  6.5 81.9 %all-gather.2.cloned.1.call-start = ((), (), s32[]{:S(2)}) async-start(), calls=%async_computation.3 | async-start | bytes 3932160 | tf_op jit(solution)/shard_map/all_gather | solution.py:30
  24.1 184.1 %reduce-scatter.2.cloned.1.call-start = ((), (), s32[]{:S(2)}) async-start(), calls=%async_computation.4 | async-start | bytes 3932160 | tf_op jit(solution)/shard_map/reduce_scatter | solution.py:40
  88.5 23.5 %copy-start.4 = (bf16[384,4096]{1,0:T(8,128)(2,1)S(1)}, bf16[384,4096]{1,0:T(8,128)(2,1)}, u32[]{:S(2)}) copy-start(bf16[384,4096]{1,0:T(8,128)(2,1)} %all-gather.2.cloned.1.call-done) | copy-start | bytes 9437188
  130.2 81.5 %copy-start.2 = (f32[128,2]{0,1:T(2,128)S(1)}, f32[128,2]{0,1:T(2,128)}, u32[]{:S(2)}) copy-start(f32[128,2]{0,1:T(2,128)} %param.8) | copy-start | bytes 3076
  130.2 81.5 %copy-start.3 = (s32[128,2]{0,1:T(2,128)S(1)}, s32[128,2]{0,1:T(2,128)}, u32[]{:S(2)}) copy-start(s32[128,2]{0,1:T(2,128)} %param.7) | copy-start | bytes 3076
  130.2 94.3 %copy-start.1 = (bf16[128,1024]{1,0:T(8,128)(2,1)S(1)}, bf16[128,1024]{1,0:T(8,128)(2,1)}, u32[]{:S(2)}) copy-start(bf16[128,1024]{1,0:T(8,128)(2,1)} %param.6) | copy-start | bytes 786436
  208.2 15.1 %all-to-all-start.1 = ((bf16[4,96,1024]{2,1,0:T(8,128)(2,1)}), bf16[4,96,1024]{2,1,0:T(8,128)(2,1)S(1)}, u32[]{:S(2)}, u32[]{:S(2)}) async-start(bf16[4,96,1024]{2,1,0:T(8,128)(2,1)} %bitcast.38), calls=%async_computation.2 | async-start | bytes 1572864 | tf_op jit(solution)/shard_map/all_to_all | solution.py:44
Sparse Core Ops, SparseCore 0:
  24.2 64.1 all-gather.1
  149.1 59.0 reduce-scatter.1
where the time goes:
time: 232 us; the launch traced here: 231 us
  waiting for transfers between devices  135 us (58%)
  matrix products  62.1 us (27%)
  blocking collectives  15.8 us (7%)
  between operations  13.5 us (6%)
  starting transfers between devices  3.54 us (2%)
    all_gather x1, waiting for transfers between devices, shards(): lax.all_gather(received.reshape(slot_total, local_width), 'etp', axis=1,...  64.3 us
    reduce_scatter x1, waiting for transfers between devices, shards(): lax.psum_scatter(partial_out, 'etp', scatter_dimension=1, tiled=True)  59.2 us
    dot_general x1, matrix products, shards(): jnp.dot(columns_in, gate_local, preferred_element_type=jnp.float32)  23.5 us
    dot_general x1, matrix products, shards(): jnp.dot(hidden, down_local, preferred_element_type=jnp.float32)  18.7 us
    dot_general x1, matrix products, shards(): up_sum = jnp.dot(columns_in, up_local, preferred_element_type=jnp.float32)  18.2 us
    all_to_all x1, blocking collectives, shards(): lax.all_to_all(dispatched, 'expert', split_axis=0, concat_axis=0, tiled=T...  15.8 us
    all_to_all x1, waiting for transfers between devices, shards(): lax.all_to_all(finished.reshape(cycle_size, CAP, local_width), 'expert',...  11.3 us
  transfers between devices with their start and end apart: 3, of which 3 were waited for; matrix products, arithmetic and copies ran while one was open for 0% of the time, Pallas kernels for 0%

commit v1 on v0

--- a/solution.py
+++ b/solution.py
@@ -1,6 +1,10 @@
+import functools
+
 import jax
 import jax.numpy as jnp
 from jax import lax
+from jax.experimental import pallas as pl
+from jax.experimental.pallas import tpu as pltpu
 from jax.sharding import PartitionSpec as P
 
 CAP = 96
@@ -53,9 +57,317 @@
     return mixed.astype(jnp.bfloat16)
 
 
+FOUR = 4
+RING_IN = 8
+RING_OUT = 5
+TILE_IN = 512
+TILE_OUT = 256
+PIECE = 512
+
+
+def partner(me, step):
+    low = (me % 2 + step % 2) % 2
+    high = (me // 2 + step // 2) % 2
+    return low + 2 * high
+
+
+def layer_kernel(
+    tok_ref, meta_ref, gate_hbm, up_hbm, down_hbm, out_ref,
+    metas, toks, chosen, pick, comb, acc_gate, acc_up, hidden,
+    ring_in, ring_out, kept, core_out, core_in, x_out, x_in, z_out, z_in,
+    sem_in, sem_out, meta_s, meta_r, z_s, z_r, x_s, x_r, ca_s, ca_r, cb_s, cb_r,
+    rc_s, rc_r, rx_s, rx_r, rz_s, rz_r,
+):
+    rows, width = tok_ref.shape
+    inner = gate_hbm.shape[2]
+    e = lax.axis_index("expert")
+    z = lax.axis_index("etp")
+    tiles_in = inner // TILE_IN
+    steps_in = FOUR * tiles_in
+    pieces = width // PIECE
+    per_piece = PIECE // TILE_OUT
+    steps_out = FOUR * width // TILE_OUT
+    order_out = (2, 3, 1, 0)
+
+    def fetch_in(t, slot):
+        row = pl.multiple_of(partner(z, t // tiles_in) * width, width)
+        col = pl.multiple_of((t % tiles_in) * TILE_IN, TILE_IN)
+        return [
+            pltpu.make_async_copy(
+                hbm.at[0, pl.ds(row, width), pl.ds(col, TILE_IN)],
+                ring_in.at[slot, k],
+                sem_in.at[slot, k],
+            )
+            for k, hbm in enumerate((gate_hbm, up_hbm))
+        ]
+
+    def fetch_out(u, slot):
+        per_chunk = width // TILE_OUT
+        index = u // per_chunk
+        step = (2 + index) % FOUR * (1 - index // 2) + (3 - index) * (index // 2)
+        col = partner(z, step) * width + (u % per_chunk) * TILE_OUT
+        return pltpu.make_async_copy(
+            down_hbm.at[0, :, pl.ds(pl.multiple_of(col, TILE_OUT), TILE_OUT)],
+            ring_out.at[slot],
+            sem_out.at[slot],
+        )
+
+    def send(source, target, s_sem, r_sem, axis, step):
+        me = e if axis == "expert" else z
+        return pltpu.make_async_remote_copy(
+            src_ref=source, dst_ref=target, send_sem=s_sem, recv_sem=r_sem,
+            device_id={axis: partner(me, step)},
+            device_id_type=pl.DeviceIdType.MESH,
+        )
+
+    for t in range(RING_IN):
+        for copy in fetch_in(t, t):
+            copy.start()
+
+    barrier = pltpu.get_barrier_semaphore()
+    for step in range(1, FOUR):
+        for axis, me in (("expert", e), ("etp", z)):
+            pl.semaphore_signal(
+                barrier, inc=1, device_id={axis: partner(me, step)},
+                device_id_type=pl.DeviceIdType.MESH,
+            )
+    pl.semaphore_wait(barrier, 2 * (FOUR - 1))
+
+    def block(i, j):
+        return tok_ref if i == 0 and j == 0 else toks.at[i, j]
+
+    meta_copies = [
+        send(meta_ref, metas.at[j], meta_s.at[j], meta_r.at[j], "expert", j)
+        for j in range(1, FOUR)
+    ]
+    z_copies = [None] + [
+        send(tok_ref, toks.at[i, 0], z_s.at[i], z_r.at[i], "etp", i)
+        for i in range(1, FOUR)
+    ]
+    x_copies = [
+        send(block(i, 0), toks.at[i, 2], x_s.at[i], x_r.at[i], "expert", 2)
+        for i in range(FOUR)
+    ]
+    ca_copies = [
+        send(block(i, 0), toks.at[i, 1], ca_s.at[i], ca_r.at[i], "expert", 1)
+        for i in range(FOUR)
+    ]
+    cb_copies = [
+        send(toks.at[i, 2], toks.at[i, 3], cb_s.at[i], cb_r.at[i], "expert", 1)
+        for i in range(FOUR)
+    ]
+    for copy in meta_copies:
+        copy.start()
+    x_copies[0].start()
+    for i in range(1, FOUR):
+        z_copies[i].start()
+    ca_copies[0].start()
+
+    for copy in meta_copies:
+        copy.wait_recv()
+    mine = e.astype(jnp.float32)
+    earlier = (
+        lax.broadcasted_iota(jnp.int32, (rows, rows), 0)
+        < lax.broadcasted_iota(jnp.int32, (rows, rows), 1)
+    ).astype(jnp.bfloat16)
+    slot_row = lax.broadcasted_iota(jnp.int32, (rows, rows), 0).astype(jnp.float32)
+    for j in range(FOUR):
+        meta = meta_ref[...] if j == 0 else metas[j]
+        first = meta[0:1, :] == mine
+        second = meta[1:2, :] == mine
+        routed = jnp.where(first, 1.0, 0.0) + jnp.where(second, 1.0, 0.0)
+        weight = jnp.where(first, meta[2:3, :], 0.0) + jnp.where(second, meta[3:4, :], 0.0)
+        slot = jnp.dot(
+            jnp.broadcast_to(routed, (16, rows)).astype(jnp.bfloat16), earlier,
+            preferred_element_type=jnp.float32,
+        )[0:1, :]
+        slot = jnp.where(routed > 0.5, slot, -1.0)
+        hit = slot_row == slot
+        pick[j] = jnp.where(hit, 1.0, 0.0).astype(jnp.bfloat16)
+        comb[j] = jnp.where(hit, weight, 0.0).T.astype(jnp.bfloat16)
+
+    for i in range(FOUR):
+        if i + 1 < FOUR:
+            z_copies[i + 1].wait_recv()
+            x_copies[i + 1].start()
+            ca_copies[i + 1].start()
+        x_copies[i].wait_recv()
+        cb_copies[i].start()
+        if i == FOUR - 1:
+            for u in range(RING_OUT):
+                fetch_out(u, u).start()
+        ca_copies[i].wait_recv()
+        cb_copies[i].wait_recv()
+        for j in range(FOUR):
+            chosen[pl.ds(j * CAP, CAP), :] = jnp.dot(
+                pick[j, 0:CAP, :], block(i, j)[...], preferred_element_type=jnp.float32
+            ).astype(jnp.bfloat16)
+
+        def in_step(n, carry, i=i):
+            t = i * tiles_in + n
+            slot = lax.rem(t, RING_IN)
+            for copy in fetch_in(t, slot):
+                copy.wait()
+            col = pl.ds(pl.multiple_of(n * TILE_IN, TILE_IN), TILE_IN)
+            gate = jnp.dot(chosen[...], ring_in[slot, 0], preferred_element_type=jnp.float32)
+            up = jnp.dot(chosen[...], ring_in[slot, 1], preferred_element_type=jnp.float32)
+            if i > 0:
+                gate = gate + acc_gate[:, col]
+                up = up + acc_up[:, col]
+            if i < FOUR - 1:
+                acc_gate[:, col] = gate
+                acc_up[:, col] = up
+            else:
+                hidden[:, col] = (gate / (1.0 + jnp.exp(-gate)) * up).astype(jnp.bfloat16)
+
+            @pl.when(t + RING_IN < steps_in)
+            def _():
+                for copy in fetch_in(t + RING_IN, slot):
+                    copy.start()
+
+            return carry
+
+        lax.fori_loop(0, tiles_in, in_step, 0)
+
+    total = FOUR * pieces
+    core_copies = [
+        send(core_out.at[s], core_in.at[s], rc_s.at[s], rc_r.at[s], "expert", 1)
+        for s in range(total)
+    ]
+    rx_copies = [
+        send(x_out.at[s], x_in.at[s], rx_s.at[s], rx_r.at[s], "expert", 2)
+        for s in range(total)
+    ]
+    rz_copies = [
+        send(z_out.at[s], z_in.at[s], rz_s.at[s], rz_r.at[s], "etp", order_out[s // pieces])
+        for s in range(total - pieces)
+    ]
+
+    def down_piece(s):
+        def out_step(q, carry):
+            u = s * per_piece + q
+            slot = lax.rem(u, RING_OUT)
+            fetch_out(u, slot).wait()
+            part = jnp.dot(
+                hidden[...], ring_out[slot], preferred_element_type=jnp.float32
+            ).astype(jnp.bfloat16)
+            col = pl.ds(pl.multiple_of(q * TILE_OUT, TILE_OUT), TILE_OUT)
+            for j in range(FOUR):
+                share = jnp.dot(
+                    comb[j, :, 0:CAP], part[j * CAP:(j + 1) * CAP, :],
+                    preferred_element_type=jnp.float32,
+                )
+                if j % 2 == 0:
+                    kept[s, j // 2, :, col] = share
+                else:
+                    core_out[s, j // 2, :, col] = share.astype(jnp.bfloat16)
+
+            @pl.when(u + RING_OUT < steps_out)
+            def _():
+                fetch_out(u + RING_OUT, slot).start()
+
+            return carry
+
+        lax.fori_loop(0, per_piece, out_step, 0)
+        core_copies[s].start()
+
+    def x_stage(s):
+        core_copies[s].wait_recv()
+        x_out[s] = (kept[s, 1] + core_in[s, 1].astype(jnp.float32)).astype(jnp.bfloat16)
+        rx_copies[s].start()
+
+    def z_stage(s):
+        rx_copies[s].wait_recv()
+        both = kept[s, 0] + core_in[s, 0].astype(jnp.float32) + x_in[s].astype(jnp.float32)
+        if s < total - pieces:
+            z_out[s] = both.astype(jnp.bfloat16)
+            rz_copies[s].start()
+        else:
+            kept[s, 0] = both
+
+    LAG = 4
+    for s in range(total):
+        down_piece(s)
+        if s >= 1:
+            x_stage(s - 1)
+        if s >= LAG:
+            z_stage(s - LAG)
+    x_stage(total - 1)
+    for s in range(total - LAG, total):
+        z_stage(s)
+    for h in range(pieces):
+        value = kept[total - pieces + h, 0]
+        for index in range(FOUR - 1):
+            s = index * pieces + h
+            rz_copies[s].wait_recv()
+            value = value + z_in[s].astype(jnp.float32)
+        out_ref[:, h * PIECE:(h + 1) * PIECE] = value.astype(jnp.bfloat16)
+    for copy in (
+        meta_copies + z_copies[1:] + x_copies + ca_copies + cb_copies
+        + core_copies + rx_copies + rz_copies
+    ):
+        copy.wait_send()
+
+
+def fused(tokens, route_ids, gate_weights, w_gate, w_up, w_down):
+    rows, width = tokens.shape
+    inner = w_gate.shape[2]
+    slots = FOUR * CAP
+    total = FOUR * width // PIECE
+    meta = jnp.concatenate(
+        [route_ids.T.astype(jnp.float32), gate_weights.T, jnp.zeros((4, rows), jnp.float32)], axis=0
+    )
+    bf, f32 = jnp.bfloat16, jnp.float32
+    dma = pltpu.SemaphoreType.DMA
+    vmem = pl.BlockSpec(memory_space=pltpu.VMEM)
+    hbm = pl.BlockSpec(memory_space=pl.ANY)
+    return pl.pallas_call(
+        layer_kernel,
+        out_shape=jax.ShapeDtypeStruct((rows, width), bf),
+        in_specs=[vmem, vmem, hbm, hbm, hbm],
+        out_specs=vmem,
+        scratch_shapes=[
+            pltpu.VMEM((FOUR, 8, rows), f32),
+            pltpu.VMEM((FOUR, FOUR, rows, width), bf),
+            pltpu.VMEM((slots, width), bf),
+            pltpu.VMEM((FOUR, rows, rows), bf),
+            pltpu.VMEM((FOUR, rows, rows), bf),
+            pltpu.VMEM((slots, inner), f32),
+            pltpu.VMEM((slots, inner), f32),
+            pltpu.VMEM((slots, inner), bf),
+            pltpu.VMEM((RING_IN, 2, width, TILE_IN), bf),
+            pltpu.VMEM((RING_OUT, inner, TILE_OUT), bf),
+            pltpu.VMEM((total, 2, rows, PIECE), f32),
+            pltpu.VMEM((total, 2, rows, PIECE), bf),
+            pltpu.VMEM((total, 2, rows, PIECE), bf),
+            pltpu.VMEM((total, rows, PIECE), bf),
+            pltpu.VMEM((total, rows, PIECE), bf),
+            pltpu.VMEM((total, rows, PIECE), bf),
+            pltpu.VMEM((total, rows, PIECE), bf),
+            dma((RING_IN, 2)), dma((RING_OUT,)),
+            dma((FOUR,)), dma((FOUR,)), dma((FOUR,)), dma((FOUR,)),
+            dma((FOUR,)), dma((FOUR,)), dma((FOUR,)), dma((FOUR,)),
+            dma((FOUR,)), dma((FOUR,)),
+            dma((total,)), dma((total,)), dma((total,)), dma((total,)),
+            dma((total,)), dma((total,)),
+        ],
+        compiler_params=pltpu.CompilerParams(
+            collective_id=0, has_side_effects=True, vmem_limit_bytes=67043328
+        ),
+    )(tokens, meta, w_gate, w_up, w_down)
+
+
+def pick_body(tokens, route_ids, gate_weights, w_gate, w_up, w_down):
+    square = lax.axis_size("expert") == FOUR and lax.axis_size("etp") == FOUR
+    whole = tokens.shape[1] % PIECE == 0 and w_gate.shape[2] % TILE_IN == 0
+    lanes = tokens.shape[0] == 128 and w_gate.shape[2] // TILE_IN * FOUR >= RING_IN
+    body = fused if square and whole and lanes else shards
+    return body(tokens, route_ids, gate_weights, w_gate, w_up, w_down)
+
+
 def solution(mesh):
     return jax.shard_map(
-        shards,
+        pick_body,
         mesh=mesh,
         in_specs=(
             P(("groups", "expert"), "etp"),

time: 232 us -> 89 us (0.38)
  waiting for transfers between devices: 135 us -> 0 us
  Pallas kernels: 0 us -> 85 us
  matrix products: 62.1 us -> 0 us
  blocking collectives: 15.8 us -> 0 us
  between operations: 13.5 us -> 0.01 us
  starting transfers between devices: 3.54 us -> 0 us
    pallas_call x0 -> x1, Pallas kernels: none -> 85 us  [fused(): pl.pallas_call(layer_kernel, out_shape=jax.ShapeDtypeStruct((rows, width)...]
    all_gather x1 -> x0, waiting for transfers between devices: 64.3 us -> none  [shards(): lax.all_gather(received.reshape(slot_total, local_width), 'etp', axis=1,...]
    dot_general x5 -> x0, matrix products: 62.1 us -> none  [the longest x1 23.5 us: shards(): jnp.dot(columns_in, gate_local, preferred_element_type=jnp.float32)]
    reduce_scatter x1 -> x0, waiting for transfers between devices: 59.2 us -> none  [shards(): lax.psum_scatter(partial_out, 'etp', scatter_dimension=1, tiled=True)]
    all_to_all x1 -> x0, blocking collectives: 15.8 us -> none  [shards(): lax.all_to_all(dispatched, 'expert', split_axis=0, concat_axis=0, tiled=T...]
    all_to_all x1 -> x0, waiting for transfers between devices: 11.3 us -> none  [shards(): lax.all_to_all(finished.reshape(cycle_size, CAP, local_width), 'expert',...]
    all_to_all x1 -> x0, starting transfers between devices: 3.49 us -> none  [shards(): lax.all_to_all(finished.reshape(cycle_size, CAP, local_width), 'expert',...]
  transfers between devices with their start and end apart: 3 -> 0, of which waited for: 3 -> 0; matrix products, arithmetic and copies ran while one was open for 0% -> 0% of each run, Pallas kernels for 0% -> 0%
where the time goes in v1:
time: 89 us; the launch traced here: 88.8 us
  Pallas kernels  85 us (96%)
  other arithmetic  2.02 us (2%)
  local copies, waits for them, and re-layouts  1.75 us (2%)
    pallas_call x1, Pallas kernels, fused(): pl.pallas_call(layer_kernel, out_shape=jax.ShapeDtypeStruct((rows, width)...  85 us

profile of v1, /device:TPU:0, one launch (start us, length us, event | category | flops | bytes accessed | tf_op | source)
XLA Modules:
  0.0 88.8 jit_solution(13351921415352996744)
XLA Ops:
  0.0 0.1 pad.2.clone
  0.1 0.7 convert_bitcast_fusion
  0.8 1.3 %maximum_maximum_fusion.meta_ref = f32[8,128]{1,0:T(8,128)} fusion(f32[2,128]{1,0:T(2,128)} %bitcast.3, f32[2,128]{1,0:T(2,128)S(1)} %convert_bitcast_fusion, f32[8]{0:T(128)S(1)} %pad.2.clone), kind=kLoop, calls=%fused_computation | loop fusion | flops 2048 | bytes 6176 | tf_op jit(solution)/shard_map/concatenate | solution.py:317
  2.1 85.0 %shard_map.64 = bf16[128,1024]{1,0:T(8,128)(2,1)} custom-call(bf16[128,1024]{1,0:T(8,128)(2,1)} %tok_ref.1, f32[8,128]{1,0:T(8,128)} %maximum_maximum_fusion.meta_ref, bf16[1,4096,3584]{2,1,0:T(8,128)(2,1)} %gate_hbm.1, bf16[1,4096,3584]{2,1,0:T(8,128)(2,1)} %up_hbm.1, bf16[1,3584,4096]{2,1,0:T(8,128)(2,1)} %down_hbm.1), custom_call_target="tpu_custom_call" | custom-call | tf_op jit(solution)/shard_map/pallas_call | solution.py:324
  87.1 1.7 %copy.8 = bf16[128,1024]{1,0:T(8,128)(2,1)} copy(bf16[128,1024]{1,0:T(8,128)(2,1)} %shard_map.64) | data formatting | bytes 524288
  (1 shorter events, 0.0 us)

commit v2 on v1

--- a/solution.py
+++ b/solution.py
@@ -1,3 +1,5 @@
+import functools
+
 import functools
 
 import jax
@@ -58,9 +60,9 @@
 
 
 FOUR = 4
-RING_IN = 8
+RING_IN = 5
 RING_OUT = 5
-TILE_IN = 512
+TILE_IN = 896
 TILE_OUT = 256
 PIECE = 512
 
@@ -95,7 +97,7 @@
         return [
             pltpu.make_async_copy(
                 hbm.at[0, pl.ds(row, width), pl.ds(col, TILE_IN)],
-                ring_in.at[slot, k],
+                ring_in.at[slot, :, pl.ds(k * TILE_IN, TILE_IN)],
                 sem_in.at[slot, k],
             )
             for k, hbm in enumerate((gate_hbm, up_hbm))
@@ -186,13 +188,18 @@
         pick[j] = jnp.where(hit, 1.0, 0.0).astype(jnp.bfloat16)
         comb[j] = jnp.where(hit, weight, 0.0).T.astype(jnp.bfloat16)
 
-    for i in range(FOUR):
-        if i + 1 < FOUR:
-            z_copies[i + 1].wait_recv()
-            x_copies[i + 1].start()
-            ca_copies[i + 1].start()
+    def pass_on(i):
+        z_copies[i].wait_recv()
+        x_copies[i].start()
+        ca_copies[i].start()
+
+    def pass_over(i):
         x_copies[i].wait_recv()
         cb_copies[i].start()
+
+    pass_on(1)
+    pass_over(0)
+    for i in range(FOUR):
         if i == FOUR - 1:
             for u in range(RING_OUT):
                 fetch_out(u, u).start()
@@ -204,13 +211,17 @@
             ).astype(jnp.bfloat16)
 
         def in_step(n, carry, i=i):
+            if i + 2 < FOUR:
+                pl.when(n == tiles_in // 2)(functools.partial(pass_on, i + 2))
+            if i + 1 < FOUR:
+                pl.when(n == tiles_in - 1)(functools.partial(pass_over, i + 1))
             t = i * tiles_in + n
             slot = lax.rem(t, RING_IN)
             for copy in fetch_in(t, slot):
                 copy.wait()
             col = pl.ds(pl.multiple_of(n * TILE_IN, TILE_IN), TILE_IN)
-            gate = jnp.dot(chosen[...], ring_in[slot, 0], preferred_element_type=jnp.float32)
-            up = jnp.dot(chosen[...], ring_in[slot, 1], preferred_element_type=jnp.float32)
+            both = jnp.dot(chosen[...], ring_in[slot], preferred_element_type=jnp.float32)
+            gate, up = both[:, :TILE_IN], both[:, TILE_IN:]
             if i > 0:
                 gate = gate + acc_gate[:, col]
                 up = up + acc_up[:, col]
@@ -243,8 +254,24 @@
         for s in range(total - pieces)
     ]
 
+    def x_stage(s):
+        core_copies[s].wait_recv()
+        x_out[s] = (kept[s, 1] + core_in[s, 1].astype(jnp.float32)).astype(jnp.bfloat16)
+        rx_copies[s].start()
+
+    def z_stage(s):
+        rx_copies[s].wait_recv()
+        both = kept[s, 0] + core_in[s, 0].astype(jnp.float32) + x_in[s].astype(jnp.float32)
+        if s < total - pieces:
+            z_out[s] = both.astype(jnp.bfloat16)
+            rz_copies[s].start()
+        else:
+            kept[s, 0] = both
+
     def down_piece(s):
         def out_step(q, carry):
+            if s >= 1:
+                pl.when(q == 1)(functools.partial(x_stage, s - 1))
             u = s * per_piece + q
             slot = lax.rem(u, RING_OUT)
             fetch_out(u, slot).wait()
@@ -271,25 +298,9 @@
         lax.fori_loop(0, per_piece, out_step, 0)
         core_copies[s].start()
 
-    def x_stage(s):
-        core_copies[s].wait_recv()
-        x_out[s] = (kept[s, 1] + core_in[s, 1].astype(jnp.float32)).astype(jnp.bfloat16)
-        rx_copies[s].start()
-
-    def z_stage(s):
-        rx_copies[s].wait_recv()
-        both = kept[s, 0] + core_in[s, 0].astype(jnp.float32) + x_in[s].astype(jnp.float32)
-        if s < total - pieces:
-            z_out[s] = both.astype(jnp.bfloat16)
-            rz_copies[s].start()
-        else:
-            kept[s, 0] = both
-
-    LAG = 4
+    LAG = 3
     for s in range(total):
         down_piece(s)
-        if s >= 1:
-            x_stage(s - 1)
         if s >= LAG:
             z_stage(s - LAG)
     x_stage(total - 1)
@@ -335,7 +346,7 @@
             pltpu.VMEM((slots, inner), f32),
             pltpu.VMEM((slots, inner), f32),
             pltpu.VMEM((slots, inner), bf),
-            pltpu.VMEM((RING_IN, 2, width, TILE_IN), bf),
+            pltpu.VMEM((RING_IN, width, 2 * TILE_IN), bf),
             pltpu.VMEM((RING_OUT, inner, TILE_OUT), bf),
             pltpu.VMEM((total, 2, rows, PIECE), f32),
             pltpu.VMEM((total, 2, rows, PIECE), bf),

time: 89 us -> 87.1 us (0.979)
  Pallas kernels: 85 us -> 83.1 us
    pallas_call x1, Pallas kernels: 85 us -> 83.1 us  [fused(): pl.pallas_call(layer_kernel, out_shape=jax.ShapeDtypeStruct((rows, width)...]
where the time goes in v2:
time: 87.1 us; the launch traced here: 86.9 us
  Pallas kernels  83.1 us (95%)
  other arithmetic  2.02 us (2%)
  local copies, waits for them, and re-layouts  1.75 us (2%)
    pallas_call x1, Pallas kernels, fused(): pl.pallas_call(layer_kernel, out_shape=jax.ShapeDtypeStruct((rows, width)...  83.1 us

profile of v2, /device:TPU:0, one launch (start us, length us, event | category | flops | bytes accessed | tf_op | source)
XLA Modules:
  0.0 86.9 jit_solution(7534807957996937842)
XLA Ops:
  0.0 0.1 pad.2.clone
  0.1 0.7 convert_bitcast_fusion
  0.8 1.3 %maximum_maximum_fusion.meta_ref = f32[8,128]{1,0:T(8,128)} fusion(f32[2,128]{1,0:T(2,128)} %bitcast.3, f32[2,128]{1,0:T(2,128)S(1)} %convert_bitcast_fusion, f32[8]{0:T(128)S(1)} %pad.2.clone), kind=kLoop, calls=%fused_computation | loop fusion | flops 2048 | bytes 6176 | tf_op jit(solution)/shard_map/concatenate | solution.py:328
  2.1 83.1 %shard_map.64 = bf16[128,1024]{1,0:T(8,128)(2,1)} custom-call(bf16[128,1024]{1,0:T(8,128)(2,1)} %tok_ref.1, f32[8,128]{1,0:T(8,128)} %maximum_maximum_fusion.meta_ref, bf16[1,4096,3584]{2,1,0:T(8,128)(2,1)} %gate_hbm.1, bf16[1,4096,3584]{2,1,0:T(8,128)(2,1)} %up_hbm.1, bf16[1,3584,4096]{2,1,0:T(8,128)(2,1)} %down_hbm.1), custom_call_target="tpu_custom_call" | custom-call | tf_op jit(solution)/shard_map/pallas_call | solution.py:335
  85.2 1.7 %copy.8 = bf16[128,1024]{1,0:T(8,128)(2,1)} copy(bf16[128,1024]{1,0:T(8,128)(2,1)} %shard_map.64) | data formatting | bytes 524288
  (1 shorter events, 0.0 us)
